TPU v7x, 32 devices: a whole 2x2x4 slice. The times are simulated.
32 devices in a mesh: groups: 2 (over x), tok: 16 (over z, y, core).
Axes of the slice: x: 2, y: 2, z: 4, core: 2. Of those that a mesh axis runs over, the one named last changes fastest.
Arguments:
- activations: bfloat16 [32, 128, 768], P(('groups', 'tok')), parts along dimension 0, may hold values from -32 to 32
- pair_repr: bfloat16 [256, 128, 128], P('groups', 'tok'), parts along dimension 0, may hold values from -6 to 6
- pair_gain: float32 [128], replicated, may hold values from 0.5 to 1.5
- bias_weight: float32 [128, 16], replicated, may hold values from -0.5 to 0.5
- proj_weight: bfloat16 [768, 3072], replicated, may hold values from -0.21875 to 0.21875
- query_bias: float32 [768], replicated, may hold values from -5 to 5
- out_weight: bfloat16 [768, 768], replicated, may hold values from -0.21875 to 0.21875
- token_mask: int32 [256], P('groups'), parts along dimension 0, may hold values 0 or 1
- out_cotangent: bfloat16 [32, 128, 768], P(('groups', 'tok')), parts along dimension 0, may hold values from -6 to 6
Outputs:
- grad_activations: bfloat16 [32, 128, 768], P(('groups', 'tok')), parts along dimension 0
- grad_pair: bfloat16 [256, 128, 128], P('groups', 'tok'), parts along dimension 0
- grad_proj: float32 [1536, 3072], P(('groups', 'tok')), parts along dimension 0
- grad_out_weight: float32 [1536, 768], P(('groups', 'tok')), parts along dimension 0
- grad_query_bias: float32 [1536], P('groups'), parts along dimension 0
- grad_bias_weight: float32 [256, 16], P('groups'), parts along dimension 0
- grad_pair_gain: float32 [256], P('groups'), parts along dimension 0
There are 2 independent parts, one for each index of `groups`. A program takes and returns all parts, laid end to end along the dimension named above; an argument that names none is the same for every part. Nothing has to cross between parts.
All inputs are finite; a program needn't handle non-finite values.
Results may differ from a plain program's by a relative error of at most 0.015.
The roundings to bfloat16 on the way count: a program that leaves them out, or rounds other values in their place, can miss the bound.
Values may be sent and summed in bfloat16 or wider, within the bound.
A program may use at most 128 MiB of HBM per device.

v0:
```python
import functools

import jax
import jax.numpy as jnp
from jax import lax
from jax.experimental import pallas as pl
from jax.experimental.pallas import tpu as pltpu
from jax.sharding import PartitionSpec as P

HEADS = 16
HD = 48
EPSILON = 1e-05
MASK_PENALTY = 10000.0
F32 = jnp.float32
BF16 = jnp.bfloat16
INNER = 4


def exchange_kernel(kinds, tok, *refs):
    count = len(kinds)
    ins, outs = refs[:count], refs[count : 2 * count]
    sends, recvs, local_sem = refs[2 * count : 3 * count], refs[3 * count : 4 * count], refs[4 * count]
    me = lax.axis_index("tok")
    group = me // INNER
    place = me % INNER
    across = place + 1 - 2 * (place % 2)
    beside = place + 2 - 4 * (place // 2)
    barrier = pltpu.get_barrier_semaphore()
    for step in range(1, tok):
        pl.semaphore_signal(barrier, inc=1, device_id={"tok": (me + step) % tok})
    pl.semaphore_wait(barrier, tok - 1)

    def send(k, slot, src, dst, peer):
        copy = pltpu.make_async_remote_copy(
            src_ref=src,
            dst_ref=dst,
            send_sem=sends[k].at[slot],
            recv_sem=recvs[k].at[slot],
            device_id={"tok": peer},
        )
        copy.start()
        return copy

    pending, relays, local = [], [], []
    for k, kind in enumerate(kinds):
        x, out = ins[k], outs[k]
        if kind == "near":
            first = send(k, 0, x, out.at[place], group * INNER + beside)
            pending.append(send(k, 1, x, out.at[place], group * INNER + across))
            relays.append((k, first, out.at[beside]))
        elif kind in ("all", "each"):
            for step in range(1, tok):
                peer = (me + step) % tok
                pending.append(send(k, step - 1, x if kind == "all" else x.at[peer], out.at[me], peer))
        elif kind == "near_each":
            for step in range(1, INNER):
                other = (place + step) % INNER
                pending.append(send(k, step - 1, x.at[other], out.at[place], group * INNER + other))
        else:
            for step in range(1, tok // INNER):
                other = (group + step) % (tok // INNER)
                pending.append(send(k, step - 1, x.at[other], out.at[group], other * INNER + place))
    for k, kind in enumerate(kinds):
        mine = {"all": me, "each": me, "near": place, "near_each": place, "far_each": group}[kind]
        own = ins[k] if kind in ("all", "near") else ins[k].at[mine]
        copy = pltpu.make_async_copy(own, outs[k].at[mine], local_sem.at[k])
        copy.start()
        local.append(copy)
    for k, first, block in relays:
        first.wait()
        pending.append(send(k, 2, block, block, group * INNER + across))
    for copy in local + pending:
        copy.wait()


def exchange(arrays, kinds, tok, collective_id):
    sizes = {"all": tok, "each": tok, "near": INNER, "near_each": INNER, "far_each": tok // INNER}
    shapes = []
    for x, kind in zip(arrays, kinds):
        block = x.shape if kind in ("all", "near") else x.shape[1:]
        shapes.append(jax.ShapeDtypeStruct((sizes[kind],) + block, x.dtype))
    sems = [pltpu.SemaphoreType.DMA((max(3, sizes[kind] - 1),)) for kind in kinds]
    return pl.pallas_call(
        functools.partial(exchange_kernel, kinds, tok),
        out_shape=shapes,
        in_specs=[pl.BlockSpec(memory_space=pltpu.VMEM)] * len(kinds),
        out_specs=[pl.BlockSpec(memory_space=pltpu.VMEM)] * len(kinds),
        scratch_shapes=sems + sems + [pltpu.SemaphoreType.DMA((len(kinds),))],
        compiler_params=pltpu.CompilerParams(
            collective_id=collective_id, has_side_effects=True, vmem_limit_bytes=40 * 2**20
        ),
        name=f"exchange_{collective_id}",
    )(*arrays)


def attention(query, keys, values, gate, grad_gated, bias_t, key_bias):
    scale = HD ** (-0.5)
    scores = jnp.einsum("hdj,hdi->hji", keys, query, preferred_element_type=F32) * scale
    scores = scores + bias_t.transpose(1, 0, 2).astype(F32) + key_bias[None, :, None]
    peak = jnp.max(scores, axis=1, keepdims=True)
    expo = jnp.exp(scores - peak)
    probs = expo / jnp.sum(expo, axis=1, keepdims=True)
    probs_b = probs.astype(BF16)
    attended = jnp.einsum("hdj,hji->hdi", values, probs_b, preferred_element_type=F32).astype(BF16)
    gate32 = gate.astype(F32)
    grad32 = grad_gated.astype(F32)
    att32 = attended.astype(F32)
    gated = (gate32 * att32).astype(BF16)
    grad_att = (grad32 * gate32).astype(BF16)
    grad_logit = (grad32 * att32 * gate32 * (1.0 - gate32)).astype(BF16)
    grad_probs = jnp.einsum("hdj,hdi->hji", values, grad_att, preferred_element_type=F32)
    grad_scores = probs * (grad_probs - jnp.sum(probs * grad_probs, axis=1, keepdims=True))
    scores_b = grad_scores.astype(BF16)
    grad_query = (jnp.einsum("hdj,hji->hdi", keys, scores_b, preferred_element_type=F32) * scale).astype(BF16)
    grad_key = (jnp.einsum("hdi,hji->hdj", query, scores_b, preferred_element_type=F32) * scale).astype(BF16)
    grad_value = jnp.einsum("hdi,hji->hdj", grad_att, probs_b, preferred_element_type=F32).astype(BF16)
    return jnp.stack([grad_query, grad_key, grad_value, grad_logit]), gated, grad_scores


def on_device(activations, pair_repr, pair_gain, bias_weight, proj_weight, query_bias, out_weight, token_mask, out_cotangent):
    samples, tokens, feature = activations.shape
    tok = lax.axis_size("tok")
    cols = pair_repr.shape[1]
    act = activations.reshape(samples * tokens, feature)
    cot = out_cotangent.reshape(samples * tokens, feature)
    pair_f = pair_repr.astype(F32)
    centred = pair_f - jnp.mean(pair_f, axis=-1, keepdims=True)
    rstd = lax.rsqrt(jnp.mean(centred * centred, axis=-1, keepdims=True) + EPSILON)
    normed = centred * rstd
    scaled = normed * pair_gain
    bias_cols = jnp.einsum("ijc,ch->jhi", scaled, bias_weight, precision=lax.Precision.HIGHEST).astype(BF16)
    outer = tok // INNER
    shard = feature // tok

    def near_blocks(x):
        blocks = x.reshape(outer, INNER, shard, samples * tokens).transpose(1, 0, 2, 3)
        return blocks.reshape(INNER, outer * shard, samples * tokens)

    bias_t, cot_near, act_near = exchange(
        (bias_cols, cot, near_blocks(act.T)), ("all", "near", "near_each"), tok, 0
    )
    bias_t = bias_t.reshape((tok * cols,) + bias_cols.shape[1:])
    proj = jnp.einsum("tf,fn->nt", act, proj_weight, preferred_element_type=F32)
    proj = proj.reshape(4, feature, samples * tokens)
    query = (proj[0] + query_bias[:, None]).astype(BF16)
    keys = proj[1].astype(BF16)
    values = proj[2].astype(BF16)
    gate = jax.nn.sigmoid(proj[3]).astype(BF16)
    grad_gated = jnp.einsum("tn,mn->mt", cot, out_weight, preferred_element_type=F32).astype(BF16)
    key_bias = (token_mask.astype(F32) - 1.0) * MASK_PENALTY

    def heads_of(x):
        return x.reshape(HEADS, HD, samples, tokens).transpose(2, 0, 1, 3)

    grads, gated, grad_scores = jax.vmap(attention, in_axes=(0, 0, 0, 0, 0, None, None))(
        heads_of(query), heads_of(keys), heads_of(values), heads_of(gate), heads_of(grad_gated), bias_t, key_bias
    )
    grad_rows = grads.transpose(1, 2, 3, 0, 4).reshape(4 * feature, samples * tokens)
    gated_t = gated.transpose(1, 2, 0, 3).reshape(feature, samples * tokens)
    score_sum = jnp.sum(grad_scores, axis=0).astype(BF16)
    outgoing = score_sum.reshape(HEADS, tok, cols, tokens).transpose(1, 2, 0, 3)
    received, rows_near, gated_near = exchange(
        (outgoing, grad_rows, near_blocks(gated_t)), ("each", "near", "near_each"), tok, 1
    )
    grad_bias = jnp.sum(received.astype(F32), axis=0)
    grad_activations = jnp.einsum("nt,fn->tf", grad_rows, proj_weight, preferred_element_type=F32).astype(BF16)
    grad_zg = jnp.einsum("jhi,ch->ijc", grad_bias, bias_weight, precision=lax.Precision.HIGHEST)
    weight_part = jnp.einsum("ijc,jhi->ch", scaled, grad_bias, precision=lax.Precision.HIGHEST)
    gain_part = jnp.sum(normed * grad_zg, axis=(0, 1))
    query_part = jnp.sum(grad_rows[:feature].astype(F32), axis=1)
    small = jnp.concatenate([query_part, weight_part.reshape(-1), gain_part])
    small = jnp.pad(small, (0, -small.size % 1024)).reshape(-1, 128)
    first = jnp.einsum("srt,snt->rn", act_near, rows_near, preferred_element_type=F32)
    second = jnp.einsum("srt,stn->rn", gated_near, cot_near, preferred_element_type=F32)
    terms = jnp.concatenate([first.astype(BF16), second.astype(BF16)], axis=1)
    terms, small = exchange((terms.reshape(outer, shard, -1), small), ("far_each", "all"), tok, 2)
    weight_grads = jnp.sum(terms.astype(F32), axis=0)
    small = jnp.sum(small, axis=0).reshape(-1)
    grad_norm = grad_zg * pair_gain
    grad_pair = (
        grad_norm
        - jnp.mean(grad_norm, axis=-1, keepdims=True)
        - normed * jnp.mean(grad_norm * normed, axis=-1, keepdims=True)
    ) * rstd
    split = feature + weight_part.size
    return (
        grad_activations.reshape(samples, tokens, feature),
        grad_pair.astype(BF16),
        weight_grads[:, : 4 * feature],
        weight_grads[:, 4 * feature :],
        small[:feature],
        small[feature:split].reshape(weight_part.shape),
        small[split : split + pair_gain.shape[0]],
    )


def solution(mesh):
    in_specs = (
        P(("groups", "tok"), None, None),
        P("groups", "tok", None),
        P(),
        P(),
        P(),
        P(),
        P(),
        P("groups"),
        P(("groups", "tok"), None, None),
    )
    out_specs = (
        P(("groups", "tok"), None, None),
        P("groups", "tok", None),
        P(("groups", "tok"), None),
        P(("groups", "tok"), None),
        P("groups"),
        P("groups", None),
        P("groups"),
    )
    return jax.shard_map(on_device, mesh=mesh, in_specs=in_specs, out_specs=out_specs, check_vma=False)
```

profile of v0, /device:TPU:5, one launch (start us, length us, event | category | flops | bytes accessed | tf_op | source)
XLA Modules:
  0.0 131.3 jit_solution(13464545769975276038)
XLA Ops:
  0.6 0.0 copy-start
  0.7 0.8 add_multiply_fusion
  1.5 0.8 add.48
  2.2 2.1 %convolution_convert_fusion.3 = bf16[768,128]{1,0:T(8,128)(2,1)} fusion(bf16[768,768]{1,0:T(8,128)(2,1)S(1)} %copy-done, bf16[1,128,768]{2,1,0:T(8,128)(2,1)} %param.17), kind=kOutput, calls=%fused_computation.19 | convolution fusion | flops 151093248 | bytes 1572864 | tf_op jit(solution)/shard_map/tn,mn->mt/dot_general | solution.py:149
  4.3 1.2 copy.24
  5.5 0.2 copy.25
  5.8 0.1 fusion.27
  5.9 0.5 copy-done.4
  6.5 0.5 fusion.13.refs_0_
  7.0 18.5 %exchange_0.1 = (bf16[16,8,16,128]{3,2,1,0:T(8,128)(2,1)S(1)}, bf16[4,128,768]{2,1,0:T(8,128)(2,1)S(1)}, bf16[4,192,128]{2,1,0:T(8,128)(2,1)S(1)}) custom-call(bf16[8,16,128]{2,1,0:T(8,128)(2,1)S(1)} %fusion.13.refs_0_, bf16[128,768]{1,0:T(8,128)(2,1)S(1)} %bitcast.96, bf16[4,192,128]{2,1,0:T(8,128)(2,1)S(1)} %bitcast.97), custom_call_target="tpu_custom_call" | custom-call | tf_op jit(solution)/shard_map/exchange_0/pallas_call | solution.py:83
  25.5 0.1 bitcast_convert_fusion
  25.6 3.8 %fusion.56 = (bf16[3072,128]{1,0:T(8,128)(2,1)S(1)}, f32[3072,128]{1,0:T(8,128)S(1)}) fusion(bf16[768,3072]{1,0:T(8,128)(2,1)} %param.13, bf16[1,128,768]{2,1,0:T(8,128)(2,1)S(1)} %copy-done.10), kind=kOutput, calls=%fused_computation.93 | convolution fusion | flops 604372992 | bytes 7274496 | tf_op jit(solution)/shard_map/tf,fn->nt/dot_general | solution.py:143
  29.4 0.7 fusion.55
  30.1 0.8 fusion.54
  30.9 0.7 fusion.5
  31.6 1.0 copy-done.3
  32.6 0.9 fusion.57
  33.6 3.0 %fusion.11 = bf16[1,1,16,48,128]{4,3,2,1,0:T(8,128)(2,1)} fusion(bf16[16,48,128]{2,1,0:T(8,128)(2,1)} %bitcast.111, bf16[16,48,128]{2,1,0:T(8,128)(2,1)} %bitcast.105, f32[16,128]{1,0:T(8,128)S(1)} %get-tuple-element.48, f32[16,128,128]{2,1,0:T(8,128)} %copy-done.3), kind=kOutput, calls=%fused_computation.23 | convolution fusion | flops 26445952 | bytes 1646592 | tf_op jit(solution)/shard_map/vmap(hdi,hji->hdj)/dot_general | solution.py:116
  36.5 2.9 %fusion.31 = (bf16[16,48,128]{2,1,0:T(8,128)(2,1)}, bf16[1,1,16,48,128]{4,3,2,1,0:T(8,128)(2,1)}) fusion(bf16[16,48,128]{2,1,0:T(8,128)(2,1)} %bitcast.112, bf16[16,48,128]{2,1,0:T(8,128)(2,1)S(1)} %bitcast.107, bf16[16,48,128]{2,1,0:T(8,128)(2,1)} %bitcast.109, f32[16,128]{1,0:T(8,128)S(1)} %get-tuple-element.48, f32[16,128,128]{2,1,0:T(8,128)} %copy-done.3), kind=kOutput, calls=%fused_computation.57 | convolution fusion | flops 27035776 | bytes 2039808 | tf_op jit(solution)/shard_map/vmap(hdj,hji->hdi)/dot_general | solution.py:104
  39.4 0.9 copy.30
  40.4 1.5 %multiply_reduce_fusion = (f32[16,128]{1,0:T(8,128)S(1)}, f32[16,128,128]{2,1,0:T(8,128)S(1)}) fusion(f32[16,128,128]{2,1,0:T(8,128)S(1)} %get-tuple-element.49, f32[16,128]{1,0:T(8,128)S(1)} %get-tuple-element.48, bf16[16,48,128]{2,1,0:T(8,128)(2,1)} %bitcast.110, bf16[16,48,128]{2,1,0:T(8,128)(2,1)} %bitcast.113, bf16[16,48,128]{2,1,0:T(8,128)(2,1)} %bitcast.106), kind=kOutput, calls=%fused_computation.30 | convolution fusion | flops 26343424 | bytes 2703360 | tf_op jit(solution)/shard_map/vmap(hdj,hdi->hji)/dot_general | solution.py:111
  41.9 0.2 multiply_convert_fusion
  42.1 0.8 copy-done.7
  42.9 0.5 fusion.10
  43.4 0.4 convert_reduce_fusion.3
  43.7 0.3 copy.29
  44.1 0.1 reduce_sum.113
  44.2 1.1 pad_maximum_fusion.1
  45.3 4.7 %fusion.12 = bf16[1,128,768]{2,1,0:T(8,128)(2,1)} fusion(bf16[3072,128]{1,0:T(8,128)(2,1)S(1)} %bitcast.92, bf16[768,3072]{1,0:T(8,128)(2,1)} %param.13), kind=kOutput, calls=%fused_computation.24 | convolution fusion | flops 604078080 | bytes 5701632 | tf_op jit(solution)/shard_map/nt,fn->tf/dot_general | solution.py:166
  50.0 29.6 %exchange_1.1 = (bf16[16,8,16,128]{3,2,1,0:T(8,128)(2,1)S(1)}, bf16[4,3072,128]{2,1,0:T(8,128)(2,1)S(1)}, bf16[4,192,128]{2,1,0:T(8,128)(2,1)S(1)}) custom-call(bf16[16,8,16,128]{3,2,1,0:T(8,128)(2,1)S(1)} %bitcast.95, bf16[3072,128]{1,0:T(8,128)(2,1)S(1)} %bitcast.93, bf16[4,192,128]{2,1,0:T(8,128)(2,1)S(1)} %bitcast.98), custom_call_target="tpu_custom_call" | custom-call | tf_op jit(solution)/shard_map/exchange_1/pallas_call | solution.py:83
  79.7 1.7 %copy-done.1 = bf16[4,3072,128]{2,1,0:T(8,128)(2,1)} copy-done((bf16[4,3072,128]{2,1,0:T(8,128)(2,1)}, bf16[4,3072,128]{2,1,0:T(8,128)(2,1)S(1)}, u32[]{:S(2)}) %copy-start.1) | copy-done | bytes 3145752
  81.3 0.3 fusion.6
  81.7 0.1 convert_reduce_fusion.1
  81.7 0.6 convolution_bitcast_fusion.3
  82.4 0.1 reshape.212
  82.5 0.8 fusion.26
  83.3 0.2 fusion.25
  83.5 0.9 copy.33
  84.4 3.1 %fusion.1 = bf16[192,3072]{1,0:T(8,128)(2,1)S(1)} fusion(bf16[4,192,128]{2,1,0:T(8,128)(2,1)S(1)} %get-tuple-element.17, bf16[4,3072,128]{2,1,0:T(8,128)(2,1)} %copy-done.1), kind=kOutput, calls=%fused_computation.2 | convolution fusion | flops 604569600 | bytes 4521984 | tf_op jit(solution)/shard_map/srt,snt->rn/dot_general | solution.py:173
  87.4 0.1 pad_maximum_fusion
  87.5 40.1 %exchange_2.1 = (bf16[4,48,3840]{2,1,0:T(8,128)(2,1)S(1)}, f32[16,24,128]{2,1,0:T(8,128)S(1)}) custom-call(bf16[4,48,3840]{2,1,0:T(8,128)(2,1)S(1)} %bitcast.94, f32[24,128]{1,0:T(8,128)S(1)} %fusion.50.refs_1_), custom_call_target="tpu_custom_call" | custom-call | tf_op jit(solution)/shard_map/exchange_2/pallas_call | solution.py:83
  127.7 0.2 convert_reduce_fusion
  128.0 0.5 slice_bitcast_fusion.1
  128.5 0.6 slice_bitcast_fusion
  129.1 0.1 reshape.214
  129.2 0.7 copy.34
  129.8 0.7 slice.58
  130.5 0.9 slice.57
  (33 shorter events, 0.2 us)
Async XLA Ops:
  0.6 1.6 %copy-start = (bf16[768,768]{1,0:T(8,128)(2,1)S(1)}, bf16[768,768]{1,0:T(8,128)(2,1)}, u32[]{:S(2)}) copy-start(bf16[768,768]{1,0:T(8,128)(2,1)} %param.15) | copy-start | bytes 3538948
  0.6 5.8 %copy-start.13 = (f32[128]{0:T(128)S(1)}, f32[128]{0:T(128)}, u32[]{:S(2)}) copy-start(f32[128]{0:T(128)} %param.11) | copy-start | bytes 1540
  0.7 6.3 %copy-start.2 = (bf16[1,128,768]{2,1,0:T(8,128)(2,1)S(1)}, bf16[1,128,768]{2,1,0:T(8,128)(2,1)}, u32[]{:S(2)}) copy-start(bf16[1,128,768]{2,1,0:T(8,128)(2,1)} %param.17) | copy-start | bytes 589828
  0.7 5.8 %copy-start.14 = (f32[128,16]{0,1:T(8,128)S(1)}, f32[128,16]{0,1:T(8,128)}, u32[]{:S(2)}) copy-start(f32[128,16]{0,1:T(8,128)} %param.12) | copy-start | bytes 24580
  0.7 4.8 %copy-start.11 = (bf16[128,8,128]{2,1,0:T(8,128)(2,1)S(1)}, bf16[128,8,128]{2,1,0:T(8,128)(2,1)}, u32[]{:S(2)}) copy-start(bf16[128,8,128]{2,1,0:T(8,128)(2,1)} %param.10) | copy-start | bytes 786436
  4.3 21.3 %copy-start.10 = (bf16[1,128,768]{2,1,0:T(8,128)(2,1)S(1)}, bf16[1,128,768]{2,1,0:T(8,128)(2,1)}, u32[]{:S(2)}) copy-start(bf16[1,128,768]{2,1,0:T(8,128)(2,1)} %param.9) | copy-start | bytes 589828
  5.7 0.7 copy-start.4
  30.1 3.5 %copy-start.8 = (bf16[768,128]{1,0:T(8,128)(2,1)}, bf16[768,128]{1,0:T(8,128)(2,1)S(1)}, u32[]{:S(2)}) copy-start(bf16[768,128]{1,0:T(8,128)(2,1)S(1)} %get-tuple-element.42) | copy-start | bytes 589828
  30.9 2.7 %copy-start.6 = (f32[768,128]{1,0:T(8,128)}, f32[768,128]{1,0:T(8,128)S(1)}, u32[]{:S(2)}) copy-start(f32[768,128]{1,0:T(8,128)S(1)} %get-tuple-element.40) | copy-start | bytes 1179652
  31.6 1.0 copy-start.3
  33.6 3.0 %copy-start.12 = (bf16[768,128]{1,0:T(8,128)(2,1)S(1)}, bf16[768,128]{1,0:T(8,128)(2,1)}, u32[]{:S(2)}) copy-start(bf16[768,128]{1,0:T(8,128)(2,1)} %convolution_convert_fusion.3) | copy-start | bytes 589828
  41.9 1.0 copy-start.7
  41.9 1.5 %copy-start.9 = (bf16[768,128]{1,0:T(8,128)(2,1)S(1)}, bf16[768,128]{1,0:T(8,128)(2,1)}, u32[]{:S(2)}) copy-start(bf16[768,128]{1,0:T(8,128)(2,1)} %copy-done.8) | copy-start | bytes 589828
  50.0 31.7 %copy-start.5 = (bf16[128,8,128]{0,2,1:T(8,128)(2,1)S(1)}, bf16[128,8,128]{0,2,1:T(8,128)(2,1)}, u32[]{:S(2)}) copy-start(bf16[128,8,128]{0,2,1:T(8,128)(2,1)} %copy-done.4) | copy-start | bytes 786436
  79.7 1.7 %copy-start.1 = (bf16[4,3072,128]{2,1,0:T(8,128)(2,1)}, bf16[4,3072,128]{2,1,0:T(8,128)(2,1)S(1)}, u32[]{:S(2)}) copy-start(bf16[4,3072,128]{2,1,0:T(8,128)(2,1)S(1)} %get-tuple-element.18) | copy-start | bytes 9437188
where the time goes:
time: 133 us; the launch traced here: 131 us
  Pallas kernels  88.3 us (66%)
  matrix products  24.8 us (19%)
  local copies, waits for them, and re-layouts  12.6 us (9%)
  other arithmetic  4.7 us (4%)
    pallas_call x3, Pallas kernels, exchange(): pl.pallas_call(functools.partial(exchange_kernel, kinds, tok), out_shape=...  88.3 us
    unnamed x34, local copies, waits for them, and re-layouts  6.94 us
    dot_general x1, matrix products, on_device(): jnp.einsum('nt,fn->tf', grad_rows, proj_weight, preferred_element_type=F32)  4.71 us
    dot_general x1, matrix products, on_device(): proj = jnp.einsum('tf,fn->nt', act, proj_weight, preferred_element_type=F32)  3.79 us
    dot_general x1, matrix products, on_device(): jnp.einsum('srt,snt->rn', act_near, rows_near, preferred_element_type=F32)  3.06 us
    dot_general x1, matrix products, attention(): jnp.einsum('hdi,hji->hdj', grad_att, probs_b, preferred_element_type=F32)  2.96 us
    dot_general x1, matrix products, attention(): jnp.einsum('hdj,hji->hdi', values, probs_b, preferred_element_type=F32)  2.88 us

commit v1 on v0

--- a/solution.py
+++ b/solution.py
@@ -117,7 +117,7 @@
     return jnp.stack([grad_query, grad_key, grad_value, grad_logit]), gated, grad_scores
 
 
-def on_device(activations, pair_repr, pair_gain, bias_weight, proj_weight, query_bias, out_weight, token_mask, out_cotangent):
+def general_plan(activations, pair_repr, pair_gain, bias_weight, proj_weight, query_bias, out_weight, token_mask, out_cotangent):
     samples, tokens, feature = activations.shape
     tok = lax.axis_size("tok")
     cols = pair_repr.shape[1]
@@ -194,6 +194,512 @@
     )
 
 
+NN = (((1,), (0,)), ((), ()))
+NT = (((1,), (1,)), ((), ()))
+TN = (((0,), (0,)), ((), ()))
+
+
+def dot(a, b, dims, precision=None):
+    return lax.dot_general(a, b, dims, precision=precision, preferred_element_type=F32)
+
+
+def fused_kernel(
+    tok,
+    act,
+    cot,
+    pair,
+    gain,
+    bias_w,
+    query_bias,
+    mask,
+    proj_hbm,
+    out_w_hbm,
+    grad_act,
+    grad_pair,
+    grad_w,
+    grad_out,
+    small_out,
+    proj_w,
+    out_w,
+    proj_t,
+    act_all,
+    cot_all,
+    act_t,
+    query_col,
+    normed,
+    rstd,
+    bias_f,
+    bias_send,
+    bias_recv,
+    q_s,
+    k_s,
+    v_s,
+    g_s,
+    gg_s,
+    ga_s,
+    gated_s,
+    probs_s,
+    rows_a,
+    rows_b,
+    rows_back,
+    term_send,
+    term_recv,
+    wout_send,
+    wout_recv,
+    score_send,
+    score_recv,
+    score_f,
+    small_a,
+    small_b,
+    recv_a,
+    recv_b,
+    local_sem,
+    act_sems,
+    bias_sems,
+    term_sems,
+    wout_sems,
+    back_sems,
+    score_sems,
+    small_sems,
+):
+    tokens, feature = act.shape
+    inner = INNER
+    planes = tok // inner
+    group_heads, head_dim = q_s.shape[0], q_s.shape[1]
+    cols = pair.shape[0]
+    channels = pair.shape[2]
+    span = group_heads * head_dim
+    window = proj_t.shape[1]
+    shard = feature // tok
+    scale = head_dim ** (-0.5)
+    me = lax.axis_index("tok")
+    plane = me // inner
+    place = me % inner
+    across = place + 1 - 2 * (place % 2)
+    beside = place + 2 - 4 * (place // 2)
+    diagonal = across + 2 - 4 * (across // 2)
+    base = pl.multiple_of((place * span) // 128 * 128, 128)
+    offset = pl.multiple_of(place * span - (place * span) // 128 * 128, 64)
+
+    load_proj = pltpu.make_async_copy(proj_hbm, proj_w, local_sem.at[0])
+    load_proj.start()
+    load_out = pltpu.make_async_copy(
+        out_w_hbm.at[pl.ds(pl.multiple_of(place * span, 64), span)], out_w, local_sem.at[1]
+    )
+    load_out.start()
+
+    barrier = pltpu.get_barrier_semaphore()
+    for step in range(1, tok):
+        pl.semaphore_signal(barrier, inc=1, device_id={"tok": (me + step) % tok})
+    pl.semaphore_wait(barrier, tok - 1)
+
+    def remote(src, dst, sems, slot, peer, arrival=None):
+        return pltpu.make_async_remote_copy(
+            src_ref=src,
+            dst_ref=dst,
+            send_sem=sems.at[0, slot],
+            recv_sem=sems.at[1, slot if arrival is None else arrival],
+            device_id={"tok": peer},
+        )
+
+    def near(where):
+        return plane * inner + where
+
+    sent = []
+    act_beside = remote(act, act_all.at[place], act_sems, 0, near(beside))
+    act_across = remote(act, act_all.at[place], act_sems, 1, near(across))
+    cot_beside = remote(cot, cot_all.at[place], act_sems, 2, near(beside))
+    cot_across = remote(cot, cot_all.at[place], act_sems, 3, near(across))
+    for copy in (act_beside, act_across, cot_beside, cot_across):
+        copy.start()
+        sent.append(copy)
+    act_all[place] = act[...]
+    cot_all[place] = cot[...]
+
+    for j in range(cols):
+        x = pair[j].astype(F32)
+        centred = x - jnp.mean(x, axis=-1, keepdims=True)
+        r = lax.rsqrt(jnp.mean(centred * centred, axis=-1, keepdims=True) + EPSILON)
+        y = centred * r
+        normed[j] = y
+        rstd[j] = r
+        part = dot(bias_w[...], y * gain[...], NT, lax.Precision.HIGHEST)
+        bias_f[pl.ds(j * HEADS, HEADS), :] = part
+    for h in range(HEADS):
+        bias_send[h // group_heads, h % group_heads] = bias_f[pl.ds(h, cols, stride=HEADS), :].astype(BF16)
+    bias_copies = []
+    for step in range(1, tok):
+        peer = (me + step) % tok
+        copy = remote(bias_send.at[peer % inner], bias_recv.at[me], bias_sems, step - 1, peer)
+        copy.start()
+        bias_copies.append(copy)
+    sent += bias_copies
+    bias_recv[me] = bias_send[place]
+
+    row = jnp.broadcast_to(query_bias[:, pl.ds(base, window)], (128, window))
+    query_col[...] = row.T
+    load_proj.wait()
+    for b in range(4):
+        proj_t[b] = proj_w[:, pl.ds(pl.multiple_of(feature * b + base, 128), window)].T
+
+    act_beside.wait_recv()
+    act_relay = remote(act_all.at[beside], act_all.at[beside], act_sems, 4, near(across))
+    act_relay.start()
+    cot_beside.wait_recv()
+    cot_relay = remote(cot_all.at[beside], cot_all.at[beside], act_sems, 5, near(across))
+    cot_relay.start()
+    sent += [act_relay, cot_relay]
+    act_across.wait_recv()
+    act_relay.wait_recv()
+    total = inner * tokens
+    acts = act_all[...].reshape(total, feature)
+    stored = (group_heads, head_dim, total)
+    for b, target in enumerate((q_s, k_s, v_s, g_s)):
+        block = dot(proj_t[b, pl.ds(offset, span), :], acts, NT)
+        if b == 0:
+            shift = query_col[pl.ds(offset, span), :]
+            block = block + jnp.concatenate([shift] * (total // 128), axis=1)
+        if b == 3:
+            block = jax.nn.sigmoid(block)
+        target[...] = block.astype(BF16).reshape(stored)
+    for i in range(inner):
+        act_t[:, i * tokens : (i + 1) * tokens] = act_all[i].T
+    cot_across.wait_recv()
+    cot_relay.wait_recv()
+    load_out.wait()
+    cots = cot_all[...].reshape(total, feature)
+    gg_s[...] = dot(out_w[...], cots, NT).astype(BF16).reshape(stored)
+    for copy in bias_copies:
+        copy.wait_recv()
+
+    key_row = jnp.broadcast_to((mask[...].astype(F32) - 1.0) * MASK_PENALTY, (tokens, tokens))
+    key_bias = key_row.T
+
+    def forward(k, carry):
+        bias = bias_recv[:, k].astype(F32).reshape(tokens, tokens)
+        for s in range(inner):
+            at = slice(s * tokens, (s + 1) * tokens)
+            query, keys, values = q_s[k, :, at], k_s[k, :, at], v_s[k, :, at]
+            scores = dot(keys, query, TN) * scale + bias + key_bias
+            expo = jnp.exp(scores - jnp.max(scores, axis=0, keepdims=True))
+            probs = expo / jnp.sum(expo, axis=0, keepdims=True)
+            probs_b = probs.astype(BF16)
+            attended = dot(values, probs_b, NN).astype(BF16).astype(F32)
+            gate32 = g_s[k, :, at].astype(F32)
+            grad32 = gg_s[k, :, at].astype(F32)
+            grad_att = (grad32 * gate32).astype(BF16)
+            gated_s[k, :, at] = (gate32 * attended).astype(BF16)
+            ga_s[k, :, at] = grad_att
+            rows_a[1, s, k] = (grad32 * attended * gate32 * (1.0 - gate32)).astype(BF16)
+            rows_a[0, s, k] = dot(grad_att, probs_b, NT).astype(BF16)
+            probs_s[k, s] = probs
+        return carry
+
+    lax.fori_loop(0, group_heads, forward, 0)
+
+    order = [planes // 2] + [o for o in range(1, planes) if o != planes // 2] + [0]
+
+    def send_terms(which, rows):
+        for o in order:
+            target = (plane + o) % planes
+            lhs = act_t[pl.ds(pl.multiple_of(target * (inner * shard), 16), inner * shard), :]
+            part = dot(lhs, rows, NT)
+            term_send[which, target] = part.astype(BF16).reshape(inner, shard, 2 * span)
+            for d in range(inner):
+                if o == 0 and d == 0:
+                    continue
+                where = (place + d) % inner
+                copy = remote(
+                    term_send.at[which, target, where],
+                    term_recv.at[which, me],
+                    term_sems,
+                    which * tok + o * inner + d,
+                    target * inner + where,
+                )
+                copy.start()
+                sent.append(copy)
+                terms.append(copy)
+        term_recv[which, me] = term_send[which, plane, place]
+
+    def send_rows(which, rows):
+        for d in range(1, inner):
+            where = (place + d) % inner
+            copy = remote(
+                rows.at[:, where],
+                rows_back.at[pl.ds(2 - 2 * which, 2), place],
+                back_sems,
+                which * inner + d,
+                near(where),
+            )
+            copy.start()
+            sent.append(copy)
+            backs.append(copy)
+        rows_back[pl.ds(2 - 2 * which, 2), place] = rows[:, place]
+
+    def side_by_side(rows):
+        return jnp.concatenate([rows[:, s].reshape(2 * span, tokens) for s in range(inner)], axis=1)
+
+    terms, backs = [], []
+    send_terms(0, side_by_side(rows_a))
+    wout_send[...] = dot(gated_s[...].reshape(span, total), cots, NN).astype(BF16).reshape(wout_send.shape)
+    wouts = []
+    for d in range(inner):
+        where = (place + d) % inner
+        copy = remote(wout_send.at[where], wout_recv.at[plane], wout_sems, d, place * inner + where, plane)
+        if d == 0:
+            @pl.when(place != plane)
+            def _():
+                copy.start()
+
+            @pl.when(place == plane)
+            def _():
+                wout_recv[plane] = wout_send[place]
+        else:
+            copy.start()
+        wouts.append(copy)
+    send_rows(0, rows_a)
+
+    def backward(k, carry):
+        summed = jnp.zeros((tokens, tokens), F32)
+        for s in range(inner):
+            at = slice(s * tokens, (s + 1) * tokens)
+            query, keys, values = q_s[k, :, at], k_s[k, :, at], v_s[k, :, at]
+            probs = probs_s[k, s]
+            grad_probs = dot(values, ga_s[k, :, at], TN)
+            grad_scores = probs * (grad_probs - jnp.sum(probs * grad_probs, axis=0, keepdims=True))
+            scores_b = grad_scores.astype(BF16)
+            rows_b[0, s, k] = (dot(keys, scores_b, NN) * scale).astype(BF16)
+            rows_b[1, s, k] = (dot(query, scores_b, NT) * scale).astype(BF16)
+            summed = summed + grad_scores
+        score_send[:, k] = summed.reshape(tok, cols, tokens).astype(BF16)
+        return carry
+
+    lax.fori_loop(0, group_heads, backward, 0)
+
+    scores = []
+    for step in range(1, tok):
+        peer = (me + step) % tok
+        copy = remote(score_send.at[peer], score_recv.at[me], score_sems, step - 1, peer)
+        copy.start()
+        scores.append(copy)
+    sent += scores
+    score_recv[me] = score_send[me]
+    send_rows(1, rows_b)
+    rows = side_by_side(rows_b)
+    send_terms(1, rows)
+    query_part = dot(jnp.ones((8, total), BF16), rows[:window], NT)
+
+    for copy in scores:
+        copy.wait_recv()
+    for q in range(inner):
+        for k in range(group_heads):
+            part = score_recv[q, k].astype(F32)
+            for i in range(1, planes):
+                part = part + score_recv[i * inner + q, k].astype(F32)
+            h = q * group_heads + k
+            score_f[pl.ds(h * cols, cols), :] = part
+    weight_part = jnp.zeros((HEADS, channels), F32)
+    gain_part = jnp.zeros((8, channels), F32)
+    for j in range(cols):
+        grad_bias = score_f[pl.ds(j, HEADS, stride=cols), :]
+        y = normed[j]
+        weight_part = weight_part + dot(grad_bias, y * gain[...], NN, lax.Precision.HIGHEST)
+        grad_zg = dot(grad_bias, bias_w[...], TN, lax.Precision.HIGHEST)
+        gain_part = gain_part + jnp.sum((y * grad_zg).reshape(tokens // 8, 8, channels), axis=0)
+        g = grad_zg * gain[...]
+        first = jnp.mean(g, axis=-1, keepdims=True)
+        second = jnp.mean(g * y, axis=-1, keepdims=True)
+        grad_pair[j] = ((g - first - y * second) * rstd[j]).astype(BF16)
+    small_a[0:HEADS, :] = weight_part
+    small_a[HEADS : HEADS + 8, :] = gain_part
+    small_a[HEADS + 8 : HEADS + 16, :] = query_part[:, :128]
+    small_a[HEADS + 16 : HEADS + 24, :] = query_part[:, 128:]
+    firsts = []
+    for d in range(1, inner):
+        where = (place + d) % inner
+        copy = remote(small_a, recv_a.at[place], small_sems, d, near(where))
+        copy.start()
+        firsts.append(copy)
+    sent += firsts
+    recv_a[place] = small_a[...]
+    for copy in firsts:
+        copy.wait_recv()
+    held = recv_a[0, 0 : HEADS + 8, :]
+    for q in range(1, inner):
+        held = held + recv_a[q, 0 : HEADS + 8, :]
+    small_b[0 : HEADS + 8, :] = held
+    for q in range(inner):
+        for half in range(2):
+            at = HEADS + 8 + 8 * half
+            small_b[HEADS + 8 + 2 * q + half : HEADS + 9 + 2 * q + half, :] = recv_a[q, at : at + 1, :]
+    seconds = []
+    for o in range(1, planes):
+        target = (plane + o) % planes
+        copy = remote(small_b, recv_b.at[plane], small_sems, inner + o, target * inner + place)
+        copy.start()
+        seconds.append(copy)
+    sent += seconds
+    recv_b[plane] = small_b[...]
+
+    for copy in backs:
+        copy.wait_recv()
+    back = rows_back[...].reshape(4 * feature, tokens)
+    for c in range(feature // 128):
+        part = dot(proj_w[c * 128 : (c + 1) * 128, :], back, NN)
+        grad_act[:, c * 128 : (c + 1) * 128] = part.T.astype(BF16)
+
+    for copy in seconds:
+        copy.wait_recv()
+    held = recv_b[0]
+    for i in range(1, planes):
+        held = held + recv_b[i]
+    small_out[...] = held
+
+    for d, copy in enumerate(wouts):
+        if d == 0:
+            @pl.when(place != plane)
+            def _():
+                copy.wait_send()
+        else:
+            copy.wait_send()
+    for o in range(planes):
+        source = (plane + o) % planes
+        copy = remote(wout_send.at[0], wout_recv.at[source], wout_sems, 0, near(across), source)
+        if o == 0:
+            @pl.when(place != plane)
+            def _():
+                copy.wait_recv()
+        else:
+            copy.wait_recv()
+
+    held = wout_recv[0].astype(F32)
+    for i in range(1, planes):
+        held = held + wout_recv[i].astype(F32)
+    grad_out[...] = held
+    for copy in terms:
+        copy.wait_recv()
+    for q in range(inner):
+        for which in range(2):
+            held = term_recv[which, q].astype(F32)
+            for i in range(1, planes):
+                held = held + term_recv[which, i * inner + q].astype(F32)
+            at = (1 - which) * 2 * span
+            grad_w[q, :, at : at + 2 * span] = held
+    for copy in sent:
+        copy.wait_send()
+
+
+def fused_plan(activations, pair_repr, pair_gain, bias_weight, proj_weight, query_bias, out_weight, token_mask, out_cotangent):
+    samples, tokens, feature = activations.shape
+    tok = lax.axis_size("tok")
+    cols, channels = pair_repr.shape[1:]
+    group_heads = HEADS // INNER
+    planes = tok // INNER
+    span = group_heads * HD
+    window = -(-span // 128) * 128
+    shard = feature // tok
+    total = INNER * tokens
+    small_rows = HEADS + 16
+
+    def vmem(*shape, dtype=BF16):
+        return pltpu.VMEM(shape, dtype)
+
+    def sems(*shape):
+        return pltpu.SemaphoreType.DMA(shape)
+
+    scratch = [
+        vmem(feature, 4 * feature),
+        vmem(span, feature),
+        vmem(4, window, feature),
+        vmem(INNER, tokens, feature),
+        vmem(INNER, tokens, feature),
+        vmem(feature, total),
+        vmem(window, 128, dtype=F32),
+        vmem(cols, tokens, channels, dtype=F32),
+        vmem(cols, tokens, 1, dtype=F32),
+        vmem(cols * HEADS, tokens, dtype=F32),
+        vmem(INNER, group_heads, cols, tokens),
+        vmem(tok, group_heads, cols, tokens),
+    ]
+    scratch += [vmem(group_heads, HD, total)] * 7
+    scratch += [
+        vmem(group_heads, INNER, tokens, tokens, dtype=F32),
+        vmem(2, INNER, group_heads, HD, tokens),
+        vmem(2, INNER, group_heads, HD, tokens),
+        vmem(4, INNER, group_heads, HD, tokens),
+        vmem(2, planes, INNER, shard, 2 * span),
+        vmem(2, tok, shard, 2 * span),
+        vmem(group_heads, HD, feature),
+        vmem(planes, HD, feature),
+        vmem(tok, group_heads, cols, tokens),
+        vmem(tok, group_heads, cols, tokens),
+        vmem(HEADS * cols, tokens, dtype=F32),
+        vmem(HEADS + 24, channels, dtype=F32),
+        vmem(small_rows, channels, dtype=F32),
+        vmem(INNER, HEADS + 24, channels, dtype=F32),
+        vmem(planes, small_rows, channels, dtype=F32),
+        sems(2),
+        sems(2, 6),
+        sems(2, tok - 1),
+        sems(2, 2 * tok),
+        sems(2, max(planes, INNER)),
+        sems(2, 2 * INNER),
+        sems(2, tok - 1),
+        sems(2, INNER + planes),
+    ]
+    in_vmem = pl.BlockSpec(memory_space=pltpu.VMEM)
+    in_any = pl.BlockSpec(memory_space=pl.ANY)
+    grad_act, grad_pair, grad_w, grad_out, small = pl.pallas_call(
+        functools.partial(fused_kernel, tok),
+        out_shape=[
+            jax.ShapeDtypeStruct((tokens, feature), BF16),
+            jax.ShapeDtypeStruct((cols, tokens, channels), BF16),
+            jax.ShapeDtypeStruct((INNER, shard, 4 * span), F32),
+            jax.ShapeDtypeStruct((shard, feature), F32),
+            jax.ShapeDtypeStruct((small_rows, channels), F32),
+        ],
+        in_specs=[in_vmem] * 7 + [in_any] * 2,
+        out_specs=[in_vmem] * 5,
+        scratch_shapes=scratch,
+        compiler_params=pltpu.CompilerParams(
+            collective_id=3, has_side_effects=True, vmem_limit_bytes=48 * 2**20
+        ),
+        name="fused",
+    )(
+        activations.reshape(tokens, feature),
+        out_cotangent.reshape(tokens, feature),
+        pair_repr.transpose(1, 0, 2),
+        pair_gain.reshape(1, channels),
+        bias_weight.T,
+        query_bias.reshape(1, feature),
+        token_mask.reshape(1, tokens),
+        proj_weight,
+        out_weight,
+    )
+    grad_w = grad_w.reshape(INNER, shard, 4, span).transpose(1, 2, 0, 3).reshape(shard, 4 * feature)
+    query_sums = small[HEADS + 8 :].reshape(INNER, window)[:, :span].reshape(feature)
+    return (
+        grad_act.reshape(samples, tokens, feature),
+        grad_pair.transpose(1, 0, 2),
+        grad_w,
+        grad_out,
+        query_sums,
+        small[:HEADS].T,
+        jnp.sum(small[HEADS : HEADS + 8], axis=0),
+    )
+
+
+def on_device(*args):
+    samples, tokens, feature = args[0].shape
+    tok = lax.axis_size("tok")
+    cols, channels = args[1].shape[1:]
+    square = tok == INNER * INNER and HEADS == tok and feature == HEADS * HD
+    tiles = tokens == 128 and channels == 128 and tok * cols == tokens and cols % 8 == 0
+    if samples == 1 and square and tiles:
+        return fused_plan(*args)
+    return general_plan(*args)
+
+
 def solution(mesh):
     in_specs = (
         P(("groups", "tok"), None, None),

time: 133 us -> 84.2 us (0.63)
  the two profiles are of different devices: /device:TPU:5 before, /device:TPU:0 now
where the time goes in v1:
time: 84.2 us; the launch traced here: 83.9 us
  Pallas kernels  69.8 us (83%)
  local copies, waits for them, and re-layouts  12.9 us (15%)
    pallas_call x1, Pallas kernels, fused_plan(): pl.pallas_call(functools.partial(fused_kernel, tok), out_shape=[jax.Shape...  69.8 us
    unnamed x16, local copies, waits for them, and re-layouts  8.32 us
    reshape x2, local copies, waits for them, and re-layouts, fused_plan(): grad_w.reshape(INNER, shard, 4, span).transpose(1, 2, 0, 3)  2.14 us

profile of v1, /device:TPU:0, one launch (start us, length us, event | category | flops | bytes accessed | tf_op | source)
XLA Modules:
  0.0 83.9 jit_solution(10224676275118125136)
XLA Ops:
  0.6 0.7 reshape.47.query_bias
  1.3 1.0 %copy.20 = bf16[128,8,128]{2,0,1:T(8,128)(2,1)S(1)} copy(bf16[128,8,128]{2,1,0:T(8,128)(2,1)} %param.10) | data formatting | bytes 524288 | tf_op args[1]
  2.3 0.0 copy-start
  2.3 1.3 %copy-done = bf16[768,768]{1,0:T(8,128)(2,1)S(1)} copy-done((bf16[768,768]{1,0:T(8,128)(2,1)S(1)}, bf16[768,768]{1,0:T(8,128)(2,1)}, u32[]{:S(2)}) %copy-start) | copy-done | bytes 1179672
  3.6 0.0 copy-start.1
  3.6 0.9 %copy-done.1 = bf16[1,128,768]{2,1,0:T(8,128)(2,1)S(1)} copy-done((bf16[1,128,768]{2,1,0:T(8,128)(2,1)S(1)}, bf16[1,128,768]{2,1,0:T(8,128)(2,1)}, u32[]{:S(2)}) %copy-start.1) | copy-done | bytes 196632
  4.5 0.0 copy-start.2
  4.5 0.9 %copy-done.2 = bf16[1,128,768]{2,1,0:T(8,128)(2,1)S(1)} copy-done((bf16[1,128,768]{2,1,0:T(8,128)(2,1)S(1)}, bf16[1,128,768]{2,1,0:T(8,128)(2,1)}, u32[]{:S(2)}) %copy-start.2) | copy-done | bytes 196632
  5.4 0.0 copy-start.3
  5.4 0.7 copy-done.3
  6.1 0.0 copy-start.4
  6.1 0.7 copy-done.4
  6.8 0.0 copy-start.5
  6.8 0.7 copy-done.5
  7.4 69.8 %fused.1 = (bf16[128,768]{1,0:T(8,128)(2,1)S(1)}, bf16[8,128,128]{2,1,0:T(8,128)(2,1)S(1)}, f32[4,48,768]{2,1,0:T(8,128)S(1)}, f32[48,768]{1,0:T(8,128)S(1)}, f32[32,128]{1,0:T(8,128)S(1)}) custom-call(bf16[128,768]{1,0:T(8,128)(2,1)S(1)} %bitcast.16, bf16[128,768]{1,0:T(8,128)(2,1)S(1)} %bitcast.17, bf16[8,128,128]{2,1,0:T(8,128)(2,1)S(1)} %bitcast.14, ...), custom_call_target="tpu_custom_call" | custom-call | tf_op jit(solution)/shard_map/fused/pallas_call | solution.py:652
  77.2 0.9 %copy.18 = bf16[128,8,128]{2,1,0:T(8,128)(2,1)} copy(bf16[128,8,128]{2,0,1:T(8,128)(2,1)S(1)} %bitcast.15) | data formatting | bytes 524288
  78.1 0.5 slice_reduce_fusion
  78.6 0.6 slice_bitcast_fusion
  79.2 0.7 reshape.53
  79.9 0.6 reshape.50
  80.5 0.5 copy.17
  81.0 1.6 %reshape.51 = f32[48,3072]{1,0:T(8,128)} reshape(f32[48,4,4,192]{3,2,1,0:T(4,128)S(1)} %copy.17) | data formatting | bytes 1179648 | tf_op jit(solution)/shard_map/reshape | solution.py:679
  82.6 0.7 copy.23
  83.2 0.7 copy.24
  (1 shorter events, 0.0 us)
Async XLA Ops:
  2.3 1.3 %copy-start = (bf16[768,768]{1,0:T(8,128)(2,1)S(1)}, bf16[768,768]{1,0:T(8,128)(2,1)}, u32[]{:S(2)}) copy-start(bf16[768,768]{1,0:T(8,128)(2,1)} %out_w_hbm.1) | copy-start | bytes 3538948
  3.6 0.9 %copy-start.1 = (bf16[1,128,768]{2,1,0:T(8,128)(2,1)S(1)}, bf16[1,128,768]{2,1,0:T(8,128)(2,1)}, u32[]{:S(2)}) copy-start(bf16[1,128,768]{2,1,0:T(8,128)(2,1)} %param.9) | copy-start | bytes 589828
  4.5 0.9 %copy-start.2 = (bf16[1,128,768]{2,1,0:T(8,128)(2,1)S(1)}, bf16[1,128,768]{2,1,0:T(8,128)(2,1)}, u32[]{:S(2)}) copy-start(bf16[1,128,768]{2,1,0:T(8,128)(2,1)} %param.17) | copy-start | bytes 589828
  5.4 0.7 copy-start.3
  6.1 0.7 copy-start.4
  6.8 0.7 copy-start.5

commit v2 on v1

--- a/solution.py
+++ b/solution.py
@@ -207,20 +207,26 @@
     tok,
     act,
     cot,
-    pair,
-    gain,
+    pair_hbm,
+    gain_hbm,
     bias_w,
-    query_bias,
-    mask,
+    query_hbm,
+    mask_hbm,
     proj_hbm,
     out_w_hbm,
     grad_act,
     grad_pair,
     grad_w,
     grad_out,
+    query_out,
     small_out,
+    gain_out,
     proj_w,
     out_w,
+    pair,
+    gain,
+    query_bias,
+    mask,
     proj_t,
     act_all,
     cot_all,
@@ -235,9 +241,11 @@
     k_s,
     v_s,
     g_s,
-    gg_s,
+    att_s,
     ga_s,
     gated_s,
+    gg_send,
+    gg_s,
     probs_s,
     rows_a,
     rows_b,
@@ -249,12 +257,14 @@
     score_send,
     score_recv,
     score_f,
+    pair_f,
     small_a,
     small_b,
     recv_a,
     recv_b,
     local_sem,
     act_sems,
+    gg_sems,
     bias_sems,
     term_sems,
     wout_sems,
@@ -266,7 +276,7 @@
     inner = INNER
     planes = tok // inner
     group_heads, head_dim = q_s.shape[0], q_s.shape[1]
-    cols = pair.shape[0]
+    cols = pair.shape[1]
     channels = pair.shape[2]
     span = group_heads * head_dim
     window = proj_t.shape[1]
@@ -281,17 +291,21 @@
     base = pl.multiple_of((place * span) // 128 * 128, 128)
     offset = pl.multiple_of(place * span - (place * span) // 128 * 128, 64)
 
-    load_proj = pltpu.make_async_copy(proj_hbm, proj_w, local_sem.at[0])
-    load_proj.start()
-    load_out = pltpu.make_async_copy(
-        out_w_hbm.at[pl.ds(pl.multiple_of(place * span, 64), span)], out_w, local_sem.at[1]
-    )
-    load_out.start()
+    def load(src, dst, slot):
+        copy = pltpu.make_async_copy(src, dst, local_sem.at[slot])
+        copy.start()
+        return copy
+
+    load_act = load(act, act_all.at[place], 0)
+    load_pair = load(pair_hbm, pair, 1)
+    load_cot = load(cot, cot_all.at[place], 2)
+    load_small = [load(gain_hbm, gain, 3), load(query_hbm, query_bias, 4), load(mask_hbm, mask, 5)]
+    load_out = load(out_w_hbm, out_w, 6)
+    load_proj = load(proj_hbm, proj_w, 7)
 
     barrier = pltpu.get_barrier_semaphore()
     for step in range(1, tok):
         pl.semaphore_signal(barrier, inc=1, device_id={"tok": (me + step) % tok})
-    pl.semaphore_wait(barrier, tok - 1)
 
     def remote(src, dst, sems, slot, peer, arrival=None):
         return pltpu.make_async_remote_copy(
@@ -306,27 +320,29 @@
         return plane * inner + where
 
     sent = []
-    act_beside = remote(act, act_all.at[place], act_sems, 0, near(beside))
-    act_across = remote(act, act_all.at[place], act_sems, 1, near(across))
-    cot_beside = remote(cot, cot_all.at[place], act_sems, 2, near(beside))
-    cot_across = remote(cot, cot_all.at[place], act_sems, 3, near(across))
-    for copy in (act_beside, act_across, cot_beside, cot_across):
-        copy.start()
-        sent.append(copy)
-    act_all[place] = act[...]
-    cot_all[place] = cot[...]
-
+    load_pair.wait()
+    for copy in load_small:
+        copy.wait()
+    gains = gain[...].reshape(1, channels)
+    x = pair[...].astype(F32).reshape(tokens * cols, channels)
+    centred = x - jnp.mean(x, axis=-1, keepdims=True)
+    r = lax.rsqrt(jnp.mean(centred * centred, axis=-1, keepdims=True) + EPSILON)
+    normed[...] = centred * r
+    rstd[...] = jnp.broadcast_to(r, (tokens * cols, channels))
     for j in range(cols):
-        x = pair[j].astype(F32)
-        centred = x - jnp.mean(x, axis=-1, keepdims=True)
-        r = lax.rsqrt(jnp.mean(centred * centred, axis=-1, keepdims=True) + EPSILON)
-        y = centred * r
-        normed[j] = y
-        rstd[j] = r
-        part = dot(bias_w[...], y * gain[...], NT, lax.Precision.HIGHEST)
+        y = normed[pl.ds(j, tokens, stride=cols), :]
+        part = dot(bias_w[...], y * gains, NT, lax.Precision.HIGHEST)
         bias_f[pl.ds(j * HEADS, HEADS), :] = part
     for h in range(HEADS):
         bias_send[h // group_heads, h % group_heads] = bias_f[pl.ds(h, cols, stride=HEADS), :].astype(BF16)
+    load_act.wait()
+    pl.semaphore_wait(barrier, tok - 1)
+    mine = act_all.at[place]
+    act_beside = remote(mine, mine, act_sems, 0, near(beside))
+    act_across = remote(mine, mine, act_sems, 1, near(across))
+    for copy in (act_beside, act_across):
+        copy.start()
+        sent.append(copy)
     bias_copies = []
     for step in range(1, tok):
         peer = (me + step) % tok
@@ -334,10 +350,30 @@
         copy.start()
         bias_copies.append(copy)
     sent += bias_copies
+    load_cot.wait()
+    load_out.wait()
+    parts = dot(out_w[...], cot_all[place], NT).astype(BF16)
+    gg_send[...] = parts.reshape(gg_send.shape)
+    gg_copies = []
+    for d in range(1, inner):
+        where = (place + d) % inner
+        copy = remote(gg_send.at[where], gg_s.at[place], gg_sems, d, near(where))
+        copy.start()
+        gg_copies.append(copy)
+    sent += gg_copies
+    mine = cot_all.at[place]
+    cot_beside = remote(mine, mine, act_sems, 2, near(beside))
+    cot_across = remote(mine, mine, act_sems, 3, near(across))
+    for copy in (cot_beside, cot_across):
+        copy.start()
+        sent.append(copy)
     bias_recv[me] = bias_send[place]
-
-    row = jnp.broadcast_to(query_bias[:, pl.ds(base, window)], (128, window))
-    query_col[...] = row.T
+    gg_s[place] = gg_send[place]
+
+    shifts = query_bias[...].reshape(1, feature)
+    row = jnp.broadcast_to(shifts, (128, feature))
+    for c in range(feature // 128):
+        query_col[c * 128 : (c + 1) * 128, :] = row[:, c * 128 : (c + 1) * 128].T
     load_proj.wait()
     for b in range(4):
         proj_t[b] = proj_w[:, pl.ds(pl.multiple_of(feature * b + base, 128), window)].T
@@ -345,10 +381,7 @@
     act_beside.wait_recv()
     act_relay = remote(act_all.at[beside], act_all.at[beside], act_sems, 4, near(across))
     act_relay.start()
-    cot_beside.wait_recv()
-    cot_relay = remote(cot_all.at[beside], cot_all.at[beside], act_sems, 5, near(across))
-    cot_relay.start()
-    sent += [act_relay, cot_relay]
+    sent.append(act_relay)
     act_across.wait_recv()
     act_relay.wait_recv()
     total = inner * tokens
@@ -357,22 +390,15 @@
     for b, target in enumerate((q_s, k_s, v_s, g_s)):
         block = dot(proj_t[b, pl.ds(offset, span), :], acts, NT)
         if b == 0:
-            shift = query_col[pl.ds(offset, span), :]
+            shift = query_col[pl.ds(pl.multiple_of(place * span, 64), span), :]
             block = block + jnp.concatenate([shift] * (total // 128), axis=1)
         if b == 3:
             block = jax.nn.sigmoid(block)
         target[...] = block.astype(BF16).reshape(stored)
-    for i in range(inner):
-        act_t[:, i * tokens : (i + 1) * tokens] = act_all[i].T
-    cot_across.wait_recv()
-    cot_relay.wait_recv()
-    load_out.wait()
-    cots = cot_all[...].reshape(total, feature)
-    gg_s[...] = dot(out_w[...], cots, NT).astype(BF16).reshape(stored)
     for copy in bias_copies:
         copy.wait_recv()
 
-    key_row = jnp.broadcast_to((mask[...].astype(F32) - 1.0) * MASK_PENALTY, (tokens, tokens))
+    key_row = jnp.broadcast_to((mask[...].reshape(1, tokens).astype(F32) - 1.0) * MASK_PENALTY, (tokens, tokens))
     key_bias = key_row.T
 
     def forward(k, carry):
@@ -383,19 +409,35 @@
             scores = dot(keys, query, TN) * scale + bias + key_bias
             expo = jnp.exp(scores - jnp.max(scores, axis=0, keepdims=True))
             probs = expo / jnp.sum(expo, axis=0, keepdims=True)
-            probs_b = probs.astype(BF16)
-            attended = dot(values, probs_b, NN).astype(BF16).astype(F32)
+            probs_s[k, s] = probs
+            attended = dot(values, probs.astype(BF16), NN).astype(BF16)
+            att_s[k, :, at] = attended
+            gated_s[k, :, at] = (g_s[k, :, at].astype(F32) * attended.astype(F32)).astype(BF16)
+        return carry
+
+    lax.fori_loop(0, group_heads, forward, 0)
+    for i in range(inner):
+        act_t[:, i * tokens : (i + 1) * tokens] = act_all[i].T
+    for copy in gg_copies:
+        copy.wait_recv()
+
+    def gates(k, carry):
+        for s in range(inner):
+            at = slice(s * tokens, (s + 1) * tokens)
             gate32 = g_s[k, :, at].astype(F32)
-            grad32 = gg_s[k, :, at].astype(F32)
+            grad32 = gg_s[s, k].astype(F32)
+            attended = att_s[k, :, at].astype(F32)
             grad_att = (grad32 * gate32).astype(BF16)
-            gated_s[k, :, at] = (gate32 * attended).astype(BF16)
             ga_s[k, :, at] = grad_att
             rows_a[1, s, k] = (grad32 * attended * gate32 * (1.0 - gate32)).astype(BF16)
-            rows_a[0, s, k] = dot(grad_att, probs_b, NT).astype(BF16)
-            probs_s[k, s] = probs
+            rows_a[0, s, k] = dot(grad_att, probs_s[k, s].astype(BF16), NT).astype(BF16)
         return carry
 
-    lax.fori_loop(0, group_heads, forward, 0)
+    lax.fori_loop(0, group_heads, gates, 0)
+    cot_beside.wait_recv()
+    cot_relay = remote(cot_all.at[beside], cot_all.at[beside], act_sems, 5, near(across))
+    cot_relay.start()
+    sent.append(cot_relay)
 
     order = [planes // 2] + [o for o in range(1, planes) if o != planes // 2] + [0]
 
@@ -441,6 +483,9 @@
 
     terms, backs = [], []
     send_terms(0, side_by_side(rows_a))
+    cot_across.wait_recv()
+    cot_relay.wait_recv()
+    cots = cot_all[...].reshape(total, feature)
     wout_send[...] = dot(gated_s[...].reshape(span, total), cots, NN).astype(BF16).reshape(wout_send.shape)
     wouts = []
     for d in range(inner):
@@ -502,14 +547,15 @@
     gain_part = jnp.zeros((8, channels), F32)
     for j in range(cols):
         grad_bias = score_f[pl.ds(j, HEADS, stride=cols), :]
-        y = normed[j]
-        weight_part = weight_part + dot(grad_bias, y * gain[...], NN, lax.Precision.HIGHEST)
+        y = normed[pl.ds(j, tokens, stride=cols), :]
+        weight_part = weight_part + dot(grad_bias, y * gains, NN, lax.Precision.HIGHEST)
         grad_zg = dot(grad_bias, bias_w[...], TN, lax.Precision.HIGHEST)
         gain_part = gain_part + jnp.sum((y * grad_zg).reshape(tokens // 8, 8, channels), axis=0)
-        g = grad_zg * gain[...]
+        g = grad_zg * gains
         first = jnp.mean(g, axis=-1, keepdims=True)
         second = jnp.mean(g * y, axis=-1, keepdims=True)
-        grad_pair[j] = ((g - first - y * second) * rstd[j]).astype(BF16)
+        pair_f[pl.ds(j, tokens, stride=cols), :] = (g - first - y * second) * rstd[pl.ds(j, tokens, stride=cols), :]
+    grad_pair[...] = pair_f[...].reshape(tokens, cols, channels).astype(BF16)
     small_a[0:HEADS, :] = weight_part
     small_a[HEADS : HEADS + 8, :] = gain_part
     small_a[HEADS + 8 : HEADS + 16, :] = query_part[:, :128]
@@ -553,7 +599,13 @@
     held = recv_b[0]
     for i in range(1, planes):
         held = held + recv_b[i]
-    small_out[...] = held
+    small_out[...] = held[0:HEADS]
+    gain_out[...] = jnp.sum(held[HEADS : HEADS + 8], axis=0)
+    pieces = []
+    for q in range(inner):
+        at = HEADS + 8 + 2 * q
+        pieces.append(jnp.concatenate([held[at : at + 1], held[at + 1 : at + 2, : span - 128]], axis=1))
+    query_out[...] = jnp.concatenate(pieces, axis=1).reshape(feature)
 
     for d, copy in enumerate(wouts):
         if d == 0:
@@ -578,15 +630,29 @@
     grad_out[...] = held
     for copy in terms:
         copy.wait_recv()
-    for q in range(inner):
-        for which in range(2):
+    for which in range(2):
+        sums = []
+        for q in range(inner):
             held = term_recv[which, q].astype(F32)
             for i in range(1, planes):
                 held = held + term_recv[which, i * inner + q].astype(F32)
-            at = (1 - which) * 2 * span
-            grad_w[q, :, at : at + 2 * span] = held
+            sums.append(held)
+        for b in range(2):
+            at = (2 - 2 * which + b) * feature
+            joined = jnp.concatenate([x[:, b * span : (b + 1) * span] for x in sums], axis=1)
+            grad_w[:, at : at + feature] = joined
     for copy in sent:
         copy.wait_send()
+
+
+def finish_kernel(*refs):
+    count = len(refs) // 2
+    ins, outs, sem = refs[:count], refs[count : 2 * count], refs[2 * count]
+    copies = [pltpu.make_async_copy(ins[i], outs[i], sem.at[i]) for i in range(count)]
+    for copy in copies:
+        copy.start()
+    for copy in copies:
+        copy.wait()
 
 
 def fused_plan(activations, pair_repr, pair_gain, bias_weight, proj_weight, query_bias, out_weight, token_mask, out_cotangent):
@@ -609,20 +675,26 @@
 
     scratch = [
         vmem(feature, 4 * feature),
-        vmem(span, feature),
+        vmem(feature, feature),
+        vmem(tokens, cols, channels),
+        vmem(channels, dtype=F32),
+        vmem(feature, dtype=F32),
+        vmem(tokens, dtype=jnp.int32),
         vmem(4, window, feature),
         vmem(INNER, tokens, feature),
         vmem(INNER, tokens, feature),
         vmem(feature, total),
-        vmem(window, 128, dtype=F32),
-        vmem(cols, tokens, channels, dtype=F32),
-        vmem(cols, tokens, 1, dtype=F32),
+        vmem(feature, 128, dtype=F32),
+        vmem(tokens * cols, channels, dtype=F32),
+        vmem(tokens * cols, channels, dtype=F32),
         vmem(cols * HEADS, tokens, dtype=F32),
         vmem(INNER, group_heads, cols, tokens),
         vmem(tok, group_heads, cols, tokens),
     ]
     scratch += [vmem(group_heads, HD, total)] * 7
     scratch += [
+        vmem(INNER, group_heads, HD, tokens),
+        vmem(INNER, group_heads, HD, tokens),
         vmem(group_heads, INNER, tokens, tokens, dtype=F32),
         vmem(2, INNER, group_heads, HD, tokens),
         vmem(2, INNER, group_heads, HD, tokens),
@@ -634,12 +706,14 @@
         vmem(tok, group_heads, cols, tokens),
         vmem(tok, group_heads, cols, tokens),
         vmem(HEADS * cols, tokens, dtype=F32),
+        vmem(tokens * cols, channels, dtype=F32),
         vmem(HEADS + 24, channels, dtype=F32),
         vmem(small_rows, channels, dtype=F32),
         vmem(INNER, HEADS + 24, channels, dtype=F32),
         vmem(planes, small_rows, channels, dtype=F32),
-        sems(2),
+        sems(8),
         sems(2, 6),
+        sems(2, INNER),
         sems(2, tok - 1),
         sems(2, 2 * tok),
         sems(2, max(planes, INNER)),
@@ -648,44 +722,54 @@
         sems(2, INNER + planes),
     ]
     in_vmem = pl.BlockSpec(memory_space=pltpu.VMEM)
-    in_any = pl.BlockSpec(memory_space=pl.ANY)
-    grad_act, grad_pair, grad_w, grad_out, small = pl.pallas_call(
+    in_hbm = pl.BlockSpec(memory_space=pltpu.HBM)
+    shapes = [
+        jax.ShapeDtypeStruct((tokens, feature), BF16),
+        jax.ShapeDtypeStruct((tokens, cols, channels), BF16),
+        jax.ShapeDtypeStruct((shard, 4 * feature), F32),
+        jax.ShapeDtypeStruct((shard, feature), F32),
+        jax.ShapeDtypeStruct((feature,), F32),
+        jax.ShapeDtypeStruct((HEADS, channels), F32),
+        jax.ShapeDtypeStruct((channels,), F32),
+    ]
+    results = pl.pallas_call(
         functools.partial(fused_kernel, tok),
-        out_shape=[
-            jax.ShapeDtypeStruct((tokens, feature), BF16),
-            jax.ShapeDtypeStruct((cols, tokens, channels), BF16),
-            jax.ShapeDtypeStruct((INNER, shard, 4 * span), F32),
-            jax.ShapeDtypeStruct((shard, feature), F32),
-            jax.ShapeDtypeStruct((small_rows, channels), F32),
-        ],
-        in_specs=[in_vmem] * 7 + [in_any] * 2,
-        out_specs=[in_vmem] * 5,
+        out_shape=shapes,
+        in_specs=[in_hbm] * 4 + [in_vmem] + [in_hbm] * 4,
+        out_specs=[in_vmem] * len(shapes),
         scratch_shapes=scratch,
         compiler_params=pltpu.CompilerParams(
-            collective_id=3, has_side_effects=True, vmem_limit_bytes=48 * 2**20
+            collective_id=3, has_side_effects=True, vmem_limit_bytes=67043328
         ),
         name="fused",
     )(
         activations.reshape(tokens, feature),
         out_cotangent.reshape(tokens, feature),
-        pair_repr.transpose(1, 0, 2),
-        pair_gain.reshape(1, channels),
+        pair_repr,
+        pair_gain,
         bias_weight.T,
-        query_bias.reshape(1, feature),
-        token_mask.reshape(1, tokens),
+        query_bias,
+        token_mask,
         proj_weight,
         out_weight,
     )
-    grad_w = grad_w.reshape(INNER, shard, 4, span).transpose(1, 2, 0, 3).reshape(shard, 4 * feature)
-    query_sums = small[HEADS + 8 :].reshape(INNER, window)[:, :span].reshape(feature)
+    results = pl.pallas_call(
+        finish_kernel,
+        out_shape=shapes,
+        in_specs=[in_vmem] * len(shapes),
+        out_specs=[in_hbm] * len(shapes),
+        scratch_shapes=[pltpu.SemaphoreType.DMA((len(shapes),))],
+        name="finish",
+    )(*results)
+    grad_act, grad_pair, grad_w, grad_out, query_sums, weight_sums, gain_sums = results
     return (
         grad_act.reshape(samples, tokens, feature),
-        grad_pair.transpose(1, 0, 2),
+        grad_pair,
         grad_w,
         grad_out,
         query_sums,
-        small[:HEADS].T,
-        jnp.sum(small[HEADS : HEADS + 8], axis=0),
+        weight_sums.T,
+        gain_sums,
     )
 
 

time: 84.2 us -> 72 us (0.86)
  local copies, waits for them, and re-layouts: 12.9 us -> 0 us
  Pallas kernels: 69.8 us -> 71.2 us
    unnamed x16 -> x0, local copies, waits for them, and re-layouts: 8.32 us -> none
    reshape x5 -> x0, local copies, waits for them, and re-layouts: 3.51 us -> none  [the longest x2 2.14 us: fused_plan(): grad_w.reshape(INNER, shard, 4, span).transpose(1, 2, 0, 3)]
    pallas_call x1 -> x2, Pallas kernels: 69.8 us -> 71.2 us  [the longest x1 68.8 us: fused_plan(): pl.pallas_call(functools.partial(fused_kernel, tok), out_shape=shapes, in...]
    transpose x2 -> x0, local copies, waits for them, and re-layouts: 1.11 us -> none  [the longest x1 0.6 us: fused_plan(): small[:HEADS]]
where the time goes in v2:
time: 72 us; the launch traced here: 71.8 us
  Pallas kernels  71.2 us (99%)
    pallas_call x1, Pallas kernels, fused_plan(): pl.pallas_call(functools.partial(fused_kernel, tok), out_shape=shapes, in...  68.8 us
    pallas_call x1, Pallas kernels, fused_plan(): pl.pallas_call(finish_kernel, out_shape=shapes, in_specs=[in_vmem] * len(...  2.41 us

profile of v2, /device:TPU:0, one launch (start us, length us, event | category | flops | bytes accessed | tf_op | source)
XLA Modules:
  0.0 71.8 jit_solution(9244211470805909828)
XLA Ops:
  0.6 68.8 %fused.1 = (bf16[128,768]{1,0:T(8,128)(2,1)}, bf16[128,8,128]{2,1,0:T(8,128)(2,1)}, f32[48,3072]{1,0:T(8,128)}, f32[48,768]{1,0:T(8,128)}, f32[768]{0:T(1024)}, /*index=5*/f32[16,128]{1,0:T(8,128)}, f32[128]{0:T(128)}) custom-call(bf16[128,768]{1,0:T(8,128)(2,1)} %bitcast.5, bf16[128,768]{1,0:T(8,128)(2,1)} %bitcast.6, bf16[128,8,128]{2,1,0:T(8,128)(2,1)} %pair_hbm.1, ...), custom_call_target="tpu_custom_call" | custom-call | tf_op jit(solution)/shard_map/fused/pallas_call | solution.py:735
  69.4 2.4 %finish.1 = (bf16[128,768]{1,0:T(8,128)(2,1)}, bf16[128,8,128]{2,1,0:T(8,128)(2,1)}, f32[48,3072]{1,0:T(8,128)}, f32[48,768]{1,0:T(8,128)}, f32[768]{0:T(1024)}, /*index=5*/f32[16,128]{1,0:T(8,128)}, f32[128]{0:T(128)}) custom-call(bf16[128,768]{1,0:T(8,128)(2,1)} %get-tuple-element.21.refs_0_, bf16[128,8,128]{2,1,0:T(8,128)(2,1)} %get-tuple-element.22.refs_1_, ...), custom_call_target="tpu_custom_call" | custom-call | tf_op jit(solution)/shard_map/finish/pallas_call | solution.py:756

commit v3 on v2

--- a/solution.py
+++ b/solution.py
@@ -249,11 +249,15 @@
     probs_s,
     rows_a,
     rows_b,
-    rows_back,
+    back_part,
+    back_send,
+    back_recv,
     term_send,
-    term_recv,
+    term_hop,
+    term_end,
     wout_send,
-    wout_recv,
+    wout_hop,
+    wout_end,
     score_send,
     score_recv,
     score_f,
@@ -301,7 +305,10 @@
     load_cot = load(cot, cot_all.at[place], 2)
     load_small = [load(gain_hbm, gain, 3), load(query_hbm, query_bias, 4), load(mask_hbm, mask, 5)]
     load_out = load(out_w_hbm, out_w, 6)
-    load_proj = load(proj_hbm, proj_w, 7)
+    load_proj = [
+        load(proj_hbm.at[:, pl.ds(pl.multiple_of(feature * b + base, 128), window)], proj_w.at[b], 7 + b)
+        for b in range(4)
+    ]
 
     barrier = pltpu.get_barrier_semaphore()
     for step in range(1, tok):
@@ -374,9 +381,9 @@
     row = jnp.broadcast_to(shifts, (128, feature))
     for c in range(feature // 128):
         query_col[c * 128 : (c + 1) * 128, :] = row[:, c * 128 : (c + 1) * 128].T
-    load_proj.wait()
     for b in range(4):
-        proj_t[b] = proj_w[:, pl.ds(pl.multiple_of(feature * b + base, 128), window)].T
+        load_proj[b].wait()
+        proj_t[b] = proj_w[b].T
 
     act_beside.wait_recv()
     act_relay = remote(act_all.at[beside], act_all.at[beside], act_sems, 4, near(across))
@@ -439,70 +446,152 @@
     cot_relay.start()
     sent.append(cot_relay)
 
-    order = [planes // 2] + [o for o in range(1, planes) if o != planes // 2] + [0]
+    lane_sems = planes + inner
+    ends = (plane == 0) | (plane == planes - 1)
+    neighbour = jnp.where(plane < planes // 2, plane + 1, plane - 1)
+
+    def turn(i):
+        return jnp.where(plane < planes // 2, planes - 1 - i, i)
+
+    def move_terms(which, target, act_on):
+        up = target > plane
+        following = jnp.where(up, plane + 1, plane - 1)
+        way = jnp.where(up, 0, 1)
+        first = (which * 3 + way) * lane_sems
+
+        @pl.when(following == target)
+        def _():
+            for d in range(inner):
+                where = (place + d) % inner
+                act_on(
+                    remote(
+                        term_send.at[which, target, where],
+                        term_end.at[which, way, place],
+                        term_sems,
+                        first + planes + d,
+                        following * inner + where,
+                        first + planes + place,
+                    )
+                )
+
+        @pl.when(following != target)
+        def _():
+            act_on(
+                remote(
+                    term_send.at[which, target],
+                    term_hop.at[which, target],
+                    term_sems,
+                    first + target,
+                    following * inner + place,
+                )
+            )
+
+    def start(copy):
+        copy.start()
 
     def send_terms(which, rows):
-        for o in order:
-            target = (plane + o) % planes
+        for i in range(planes):
+            target = turn(i)
             lhs = act_t[pl.ds(pl.multiple_of(target * (inner * shard), 16), inner * shard), :]
             part = dot(lhs, rows, NT)
             term_send[which, target] = part.astype(BF16).reshape(inner, shard, 2 * span)
-            for d in range(inner):
-                if o == 0 and d == 0:
-                    continue
-                where = (place + d) % inner
-                copy = remote(
-                    term_send.at[which, target, where],
-                    term_recv.at[which, me],
-                    term_sems,
-                    which * tok + o * inner + d,
-                    target * inner + where,
-                )
-                copy.start()
-                sent.append(copy)
-                terms.append(copy)
-        term_recv[which, me] = term_send[which, plane, place]
-
-    def send_rows(which, rows):
+
+            @pl.when(ends & (target != plane) & (target != neighbour))
+            def _():
+                move_terms(which, target, start)
+
+        first = (which * 3 + 2) * lane_sems + planes
         for d in range(1, inner):
             where = (place + d) % inner
             copy = remote(
-                rows.at[:, where],
-                rows_back.at[pl.ds(2 - 2 * which, 2), place],
-                back_sems,
-                which * inner + d,
+                term_send.at[which, plane, where],
+                term_end.at[which, 2, place],
+                term_sems,
+                first + d,
                 near(where),
+                first + place,
             )
             copy.start()
             sent.append(copy)
-            backs.append(copy)
-        rows_back[pl.ds(2 - 2 * which, 2), place] = rows[:, place]
+        term_end[which, 2, place] = term_send[which, plane, place]
+
+    def relay_terms(which, i):
+        target = turn(i)
+
+        @pl.when(jnp.logical_not(ends) & (target != plane))
+        def _():
+            way = jnp.where(target > plane, 0, 1)
+            slot = (which * 3 + way) * lane_sems + target
+            remote(
+                term_send.at[which, target], term_hop.at[which, target], term_sems, slot, near(across)
+            ).wait_recv()
+            held = term_send[which, target].astype(F32) + term_hop[which, target].astype(F32)
+            term_send[which, target] = held.astype(BF16)
+            move_terms(which, target, start)
+
+    def settle_terms(which):
+        for i in range(planes):
+            target = turn(i)
+
+            @pl.when(target != plane)
+            def _():
+                move_terms(which, target, lambda copy: copy.wait_send())
+
+    def ended_terms(which, way):
+        first = (which * 3 + way) * lane_sems + planes
+        for q in range(inner):
+            copy = remote(
+                term_send.at[which, 0, 0], term_end.at[which, way, q], term_sems, 0, near(across), first + q
+            )
+            if way == 2:
+                pl.when(place != q)(copy.wait_recv)
+            else:
+                copy.wait_recv()
+
+    def late_terms(which):
+        @pl.when(ends)
+        def _():
+            move_terms(which, neighbour, start)
+
+    def move_wout(k, act_on):
+        up = place > plane
+        following = jnp.where(up, plane + 1, plane - 1)
+        way = jnp.where(up, 0, 1)
+
+        @pl.when((place != plane) & (following == place))
+        def _():
+            act_on(remote(wout_send.at[k], wout_end.at[way], wout_sems, 3 + k, following * inner + k, way))
+
+        @pl.when((place != plane) & (following != place))
+        def _():
+            act_on(remote(wout_send.at[k], wout_hop.at[k], wout_sems, 3 + k, following * inner + place))
+
+        @pl.when((place == plane) & (place != k))
+        def _():
+            act_on(remote(wout_send.at[k], wout_end.at[2], wout_sems, 3 + k, near(k), 2))
+
+    def relay_wout(k):
+        @pl.when(jnp.logical_not(wout_first))
+        def _():
+            remote(wout_send.at[k], wout_hop.at[k], wout_sems, 3 + k, near(across)).wait_recv()
+            wout_send[k] = (wout_send[k].astype(F32) + wout_hop[k].astype(F32)).astype(BF16)
+            move_wout(k, start)
 
     def side_by_side(rows):
         return jnp.concatenate([rows[:, s].reshape(2 * span, tokens) for s in range(inner)], axis=1)
 
-    terms, backs = [], []
     send_terms(0, side_by_side(rows_a))
     cot_across.wait_recv()
     cot_relay.wait_recv()
     cots = cot_all[...].reshape(total, feature)
     wout_send[...] = dot(gated_s[...].reshape(span, total), cots, NN).astype(BF16).reshape(wout_send.shape)
-    wouts = []
-    for d in range(inner):
-        where = (place + d) % inner
-        copy = remote(wout_send.at[where], wout_recv.at[plane], wout_sems, d, place * inner + where, plane)
-        if d == 0:
-            @pl.when(place != plane)
-            def _():
-                copy.start()
-
-            @pl.when(place == plane)
-            def _():
-                wout_recv[plane] = wout_send[place]
-        else:
-            copy.start()
-        wouts.append(copy)
-    send_rows(0, rows_a)
+
+    @pl.when(place == plane)
+    def _():
+        wout_end[2] = wout_send[place]
+
+    wout_first = ends | (place == plane)
+
 
     def backward(k, carry):
         summed = jnp.zeros((tokens, tokens), F32)
@@ -529,9 +618,18 @@
         scores.append(copy)
     sent += scores
     score_recv[me] = score_send[me]
-    send_rows(1, rows_b)
+    relay_terms(0, 0)
+    relay_terms(0, 1)
     rows = side_by_side(rows_b)
     send_terms(1, rows)
+
+    @pl.when(wout_first)
+    def _():
+        for k in range(group_heads):
+            move_wout(k, start)
+
+    for i in range(2, planes):
+        relay_terms(0, i)
     query_part = dot(jnp.ones((8, total), BF16), rows[:window], NT)
 
     for copy in scores:
@@ -587,13 +685,33 @@
     sent += seconds
     recv_b[plane] = small_b[...]
 
+    late_terms(0)
+    late_terms(1)
+    relay_terms(1, 0)
+    relay_terms(1, 1)
+    weights = jnp.concatenate([proj_t[b, pl.ds(offset, span), :] for b in range(4)], axis=0)
+
+    def back_of(first, second):
+        columns = []
+        for s in (first, second):
+            both = [x[:, s].reshape(2 * span, tokens) for x in (rows_b, rows_a)]
+            columns.append(jnp.concatenate(both, axis=0))
+        return dot(jnp.concatenate(columns, axis=1), weights, TN)
+
+    back_send[0:2] = back_of(diagonal, across).astype(BF16).reshape(2, tokens, feature)
+    backs = [remote(back_send.at[i], back_recv.at[i], back_sems, i, near(across)) for i in range(2)]
     for copy in backs:
-        copy.wait_recv()
-    back = rows_back[...].reshape(4 * feature, tokens)
-    for c in range(feature // 128):
-        part = dot(proj_w[c * 128 : (c + 1) * 128, :], back, NN)
-        grad_act[:, c * 128 : (c + 1) * 128] = part.T.astype(BF16)
-
+        copy.start()
+    back_part[...] = back_of(beside, place).reshape(2, tokens, feature)
+    backs[0].wait_recv()
+    back_send[2] = (back_part[0] + back_recv[0].astype(F32)).astype(BF16)
+    backs.append(remote(back_send.at[2], back_recv.at[2], back_sems, 2, near(beside)))
+    backs[2].start()
+    sent += backs
+    for i in range(2, planes):
+        relay_terms(1, i)
+    for k in range(group_heads):
+        relay_wout(k)
     for copy in seconds:
         copy.wait_recv()
     held = recv_b[0]
@@ -607,35 +725,36 @@
         pieces.append(jnp.concatenate([held[at : at + 1], held[at + 1 : at + 2, : span - 128]], axis=1))
     query_out[...] = jnp.concatenate(pieces, axis=1).reshape(feature)
 
-    for d, copy in enumerate(wouts):
-        if d == 0:
-            @pl.when(place != plane)
-            def _():
-                copy.wait_send()
-        else:
-            copy.wait_send()
-    for o in range(planes):
-        source = (plane + o) % planes
-        copy = remote(wout_send.at[0], wout_recv.at[source], wout_sems, 0, near(across), source)
-        if o == 0:
-            @pl.when(place != plane)
-            def _():
-                copy.wait_recv()
-        else:
-            copy.wait_recv()
-
-    held = wout_recv[0].astype(F32)
-    for i in range(1, planes):
-        held = held + wout_recv[i].astype(F32)
-    grad_out[...] = held
-    for copy in terms:
+    for copy in backs[1:]:
         copy.wait_recv()
+    held = back_part[1] + back_recv[1].astype(F32) + back_recv[2].astype(F32)
+    grad_act[...] = held.astype(BF16)
+
+    def ended_wout(way):
+        remote(wout_send.at[0], wout_end.at[way], wout_sems, 0, near(across), way).wait_recv()
+
+    pl.when(plane > 0)(lambda: ended_wout(0))
+    pl.when(plane < planes - 1)(lambda: ended_wout(1))
+    pl.when(place != plane)(lambda: ended_wout(2))
+    grad_out[...] = wout_end[2].astype(F32)
+
+    @pl.when(plane > 0)
+    def _():
+        grad_out[...] += wout_end[0].astype(F32)
+
+    @pl.when(plane < planes - 1)
+    def _():
+        grad_out[...] += wout_end[1].astype(F32)
+
     for which in range(2):
+        ended_terms(which, 2)
+        pl.when(plane > 0)(lambda: ended_terms(which, 0))
+        pl.when(plane < planes - 1)(lambda: ended_terms(which, 1))
         sums = []
         for q in range(inner):
-            held = term_recv[which, q].astype(F32)
-            for i in range(1, planes):
-                held = held + term_recv[which, i * inner + q].astype(F32)
+            held = term_end[which, 2, q].astype(F32)
+            for there, way in ((plane > 0, 0), (plane < planes - 1, 1)):
+                held = held + jnp.where(there, term_end[which, way, q].astype(F32), 0.0)
             sums.append(held)
         for b in range(2):
             at = (2 - 2 * which + b) * feature
@@ -643,6 +762,10 @@
             grad_w[:, at : at + feature] = joined
     for copy in sent:
         copy.wait_send()
+    for k in range(group_heads):
+        move_wout(k, lambda copy: copy.wait_send())
+    for which in range(2):
+        settle_terms(which)
 
 
 def finish_kernel(*refs):
@@ -674,7 +797,7 @@
         return pltpu.SemaphoreType.DMA(shape)
 
     scratch = [
-        vmem(feature, 4 * feature),
+        vmem(4, feature, window),
         vmem(feature, feature),
         vmem(tokens, cols, channels),
         vmem(channels, dtype=F32),
@@ -698,11 +821,15 @@
         vmem(group_heads, INNER, tokens, tokens, dtype=F32),
         vmem(2, INNER, group_heads, HD, tokens),
         vmem(2, INNER, group_heads, HD, tokens),
-        vmem(4, INNER, group_heads, HD, tokens),
+        vmem(2, tokens, feature, dtype=F32),
+        vmem(3, tokens, feature),
+        vmem(3, tokens, feature),
         vmem(2, planes, INNER, shard, 2 * span),
-        vmem(2, tok, shard, 2 * span),
+        vmem(2, planes, INNER, shard, 2 * span),
+        vmem(2, 3, INNER, shard, 2 * span),
         vmem(group_heads, HD, feature),
-        vmem(planes, HD, feature),
+        vmem(group_heads, HD, feature),
+        vmem(3, HD, feature),
         vmem(tok, group_heads, cols, tokens),
         vmem(tok, group_heads, cols, tokens),
         vmem(HEADS * cols, tokens, dtype=F32),
@@ -711,13 +838,13 @@
         vmem(small_rows, channels, dtype=F32),
         vmem(INNER, HEADS + 24, channels, dtype=F32),
         vmem(planes, small_rows, channels, dtype=F32),
-        sems(8),
+        sems(11),
         sems(2, 6),
         sems(2, INNER),
         sems(2, tok - 1),
-        sems(2, 2 * tok),
-        sems(2, max(planes, INNER)),
-        sems(2, 2 * INNER),
+        sems(2, 6 * (planes + INNER)),
+        sems(2, 3 + group_heads),
+        sems(2, 3),
         sems(2, tok - 1),
         sems(2, INNER + planes),
     ]

time: 72 us -> 64 us (0.89)
  the two profiles are of different devices: /device:TPU:0 before, /device:TPU:5 now
where the time goes in v3:
time: 64 us; the launch traced here: 63.8 us
  Pallas kernels  63.1 us (99%)
  between operations  0.64 us (1%)
    pallas_call x1, Pallas kernels, fused_plan(): pl.pallas_call(functools.partial(fused_kernel, tok), out_shape=shapes, in...  60.7 us
    pallas_call x1, Pallas kernels, fused_plan(): pl.pallas_call(finish_kernel, out_shape=shapes, in_specs=[in_vmem] * len(...  2.41 us

profile of v3, /device:TPU:5, one launch (start us, length us, event | category | flops | bytes accessed | tf_op | source)
XLA Modules:
  0.0 63.8 jit_solution(12821206696683976223)
XLA Ops:
  0.6 60.7 %fused.1 = (bf16[128,768]{1,0:T(8,128)(2,1)}, bf16[128,8,128]{2,1,0:T(8,128)(2,1)}, f32[48,3072]{1,0:T(8,128)}, f32[48,768]{1,0:T(8,128)}, f32[768]{0:T(1024)}, /*index=5*/f32[16,128]{1,0:T(8,128)}, f32[128]{0:T(128)}) custom-call(bf16[128,768]{1,0:T(8,128)(2,1)} %bitcast.5, bf16[128,768]{1,0:T(8,128)(2,1)} %bitcast.6, bf16[128,8,128]{2,1,0:T(8,128)(2,1)} %pair_hbm.1, ...), custom_call_target="tpu_custom_call" | custom-call | tf_op jit(solution)/shard_map/fused/pallas_call | solution.py:862
  61.4 2.4 %finish.1 = (bf16[128,768]{1,0:T(8,128)(2,1)}, bf16[128,8,128]{2,1,0:T(8,128)(2,1)}, f32[48,3072]{1,0:T(8,128)}, f32[48,768]{1,0:T(8,128)}, f32[768]{0:T(1024)}, /*index=5*/f32[16,128]{1,0:T(8,128)}, f32[128]{0:T(128)}) custom-call(bf16[128,768]{1,0:T(8,128)(2,1)} %get-tuple-element.21.refs_0_, bf16[128,8,128]{2,1,0:T(8,128)(2,1)} %get-tuple-element.22.refs_1_, ...), custom_call_target="tpu_custom_call" | custom-call | tf_op jit(solution)/shard_map/finish/pallas_call | solution.py:883

commit v4 on v3

--- a/solution.py
+++ b/solution.py
@@ -500,6 +500,7 @@
             def _():
                 move_terms(which, target, start)
 
+    def own_terms(which):
         first = (which * 3 + 2) * lane_sems + planes
         for d in range(1, inner):
             where = (place + d) % inner
@@ -665,6 +666,8 @@
         copy.start()
         firsts.append(copy)
     sent += firsts
+    relay_terms(1, 0)
+    relay_terms(1, 1)
     recv_a[place] = small_a[...]
     for copy in firsts:
         copy.wait_recv()
@@ -687,8 +690,8 @@
 
     late_terms(0)
     late_terms(1)
-    relay_terms(1, 0)
-    relay_terms(1, 1)
+    own_terms(0)
+    own_terms(1)
     weights = jnp.concatenate([proj_t[b, pl.ds(offset, span), :] for b in range(4)], axis=0)
 
     def back_of(first, second):

time: 64 us -> 58.8 us (0.919)
  Pallas kernels: 63.1 us -> 57.7 us
    pallas_call x1, Pallas kernels: 60.7 us -> 55.3 us  [fused_plan(): pl.pallas_call(functools.partial(fused_kernel, tok), out_shape=shapes, in...]
where the time goes in v4:
time: 58.8 us; the launch traced here: 58.4 us
  Pallas kernels  57.7 us (98%)
  between operations  0.64 us (1%)
    pallas_call x1, Pallas kernels, fused_plan(): pl.pallas_call(functools.partial(fused_kernel, tok), out_shape=shapes, in...  55.3 us
    pallas_call x1, Pallas kernels, fused_plan(): pl.pallas_call(finish_kernel, out_shape=shapes, in_specs=[in_vmem] * len(...  2.41 us

profile of v4, /device:TPU:5, one launch (start us, length us, event | category | flops | bytes accessed | tf_op | source)
XLA Modules:
  0.0 58.4 jit_solution(16883048287476552516)
XLA Ops:
  0.6 55.3 %fused.1 = (bf16[128,768]{1,0:T(8,128)(2,1)}, bf16[128,8,128]{2,1,0:T(8,128)(2,1)}, f32[48,3072]{1,0:T(8,128)}, f32[48,768]{1,0:T(8,128)}, f32[768]{0:T(1024)}, /*index=5*/f32[16,128]{1,0:T(8,128)}, f32[128]{0:T(128)}) custom-call(bf16[128,768]{1,0:T(8,128)(2,1)} %bitcast.5, bf16[128,768]{1,0:T(8,128)(2,1)} %bitcast.6, bf16[128,8,128]{2,1,0:T(8,128)(2,1)} %pair_hbm.1, ...), custom_call_target="tpu_custom_call" | custom-call | tf_op jit(solution)/shard_map/fused/pallas_call | solution.py:865
  56.0 2.4 %finish.1 = (bf16[128,768]{1,0:T(8,128)(2,1)}, bf16[128,8,128]{2,1,0:T(8,128)(2,1)}, f32[48,3072]{1,0:T(8,128)}, f32[48,768]{1,0:T(8,128)}, f32[768]{0:T(1024)}, /*index=5*/f32[16,128]{1,0:T(8,128)}, f32[128]{0:T(128)}) custom-call(bf16[128,768]{1,0:T(8,128)(2,1)} %get-tuple-element.21.refs_0_, bf16[128,8,128]{2,1,0:T(8,128)(2,1)} %get-tuple-element.22.refs_1_, ...), custom_call_target="tpu_custom_call" | custom-call | tf_op jit(solution)/shard_map/finish/pallas_call | solution.py:886

commit v5 on v4

--- a/solution.py
+++ b/solution.py
@@ -629,8 +629,6 @@
         for k in range(group_heads):
             move_wout(k, start)
 
-    for i in range(2, planes):
-        relay_terms(0, i)
     query_part = dot(jnp.ones((8, total), BF16), rows[:window], NT)
 
     for copy in scores:
@@ -666,6 +664,8 @@
         copy.start()
         firsts.append(copy)
     sent += firsts
+    for i in range(2, planes):
+        relay_terms(0, i)
     relay_terms(1, 0)
     relay_terms(1, 1)
     recv_a[place] = small_a[...]

time: 58.8 us -> 58.5 us (level)
  no operation moved by 1% of the time
where the time goes in v5:
time: 58.5 us; the launch traced here: 58.2 us
  Pallas kernels  57.6 us (98%)
  between operations  0.64 us (1%)
    pallas_call x1, Pallas kernels, fused_plan(): pl.pallas_call(functools.partial(fused_kernel, tok), out_shape=shapes, in...  55.2 us
    pallas_call x1, Pallas kernels, fused_plan(): pl.pallas_call(finish_kernel, out_shape=shapes, in_specs=[in_vmem] * len(...  2.41 us

profile of v5, /device:TPU:5, one launch (start us, length us, event | category | flops | bytes accessed | tf_op | source)
XLA Modules:
  0.0 58.2 jit_solution(144730893292397574)
XLA Ops:
  0.6 55.2 %fused.1 = (bf16[128,768]{1,0:T(8,128)(2,1)}, bf16[128,8,128]{2,1,0:T(8,128)(2,1)}, f32[48,3072]{1,0:T(8,128)}, f32[48,768]{1,0:T(8,128)}, f32[768]{0:T(1024)}, /*index=5*/f32[16,128]{1,0:T(8,128)}, f32[128]{0:T(128)}) custom-call(bf16[128,768]{1,0:T(8,128)(2,1)} %bitcast.5, bf16[128,768]{1,0:T(8,128)(2,1)} %bitcast.6, bf16[128,8,128]{2,1,0:T(8,128)(2,1)} %pair_hbm.1, ...), custom_call_target="tpu_custom_call" | custom-call | tf_op jit(solution)/shard_map/fused/pallas_call | solution.py:865
  55.8 2.4 %finish.1 = (bf16[128,768]{1,0:T(8,128)(2,1)}, bf16[128,8,128]{2,1,0:T(8,128)(2,1)}, f32[48,3072]{1,0:T(8,128)}, f32[48,768]{1,0:T(8,128)}, f32[768]{0:T(1024)}, /*index=5*/f32[16,128]{1,0:T(8,128)}, f32[128]{0:T(128)}) custom-call(bf16[128,768]{1,0:T(8,128)(2,1)} %get-tuple-element.21.refs_0_, bf16[128,8,128]{2,1,0:T(8,128)(2,1)} %get-tuple-element.22.refs_1_, ...), custom_call_target="tpu_custom_call" | custom-call | tf_op jit(solution)/shard_map/finish/pallas_call | solution.py:886
